TPU v7x, 256 devices: a whole 4x4x8 slice. The times are simulated.
256 devices in a mesh: dp: 8 (over y, core), expert: 8 (over z), tile: 4 (over x).
Axes of the slice: x: 4, y: 4, z: 8, core: 2. Of those that a mesh axis runs over, the one named last changes fastest.
Arguments:
- tokens: bfloat16 [4096, 4096], P(('dp', 'expert'), 'tile'), may hold values from -6 to 6
- hidden: bfloat16 [4096, 2, 7168], P(('dp', 'expert'), None, 'tile'), may hold values from -6 to 6
- routes: int32 [4096, 2], P(('dp', 'expert')), may hold values from 0 to 7, all different within a row; in each aligned block of 64 rows (0 to 63, 64 to 127, ...) at most 24 rows name the same one
- lengths: int32 [64], P(('dp', 'expert')), may hold values from 1 to 64, as said below
Outputs:
- hessian_in: float32 [8, 4096, 4096], P('expert', 'tile', 'dp')
- hessian_down: float32 [8, 7168, 7168], P('expert', 'tile', 'dp')
Inputs may be any that keep to these rules, and one draw needn't show every extreme that they name: `routes`: in each aligned block of 64 rows (the rows of one group) no expert is named by more than 24 rows, a bound that some block reaches. The live rows of group g are its first lengths[g] rows; the last group is full.
All inputs are finite; a program needn't handle non-finite values.
Results may differ from a plain program's by a relative error of at most 0.0003.
Values may be sent and summed in bfloat16 or wider, within the bound.
A program may use at most 64 MiB of HBM per device.

v0:
```python
import jax
import jax.numpy as jnp
from jax import lax
from jax.sharding import PartitionSpec as P


def sent_together(arrays, axis, split_dim, concat_dim, along):
    widths = [a.shape[along] for a in arrays]
    both = jnp.concatenate(arrays, axis=along)
    out = lax.all_to_all(both, axis, split_axis=split_dim, concat_axis=concat_dim, tiled=True)
    return tuple(jnp.split(out, [sum(widths[:k]) for k in range(1, len(widths))], axis=along))


def from_everyone(value, axis):
    copies = jnp.broadcast_to(value, (lax.axis_size(axis), *value.shape))
    return lax.all_to_all(copies, axis, split_axis=0, concat_axis=0, tiled=True)


def of_everyone(value, axis):
    everything = from_everyone(value, axis)
    return jnp.sum(everything, axis=0)


def side_by_side(arrays, axis, dim, along):
    ends, at = ([], 0)
    for a in arrays[:-1]:
        at += a.shape[along]
        ends.append(at)
    both = jnp.concatenate(arrays, axis=along)
    return tuple(jnp.split(lax.all_gather(both, axis, axis=dim, tiled=True), ends, axis=along))


def contract(left, right):
    return lax.dot_general(
        left, right, (((0,), (0,)), ((), ())), preferred_element_type=jnp.float32
    )


def dispatch_tables(routes, live_count, experts, share_size, senders):
    token_count = routes.shape[0]
    top_count = routes.shape[1]
    flat_routes = routes.reshape(token_count * top_count)
    pair_index = jnp.arange(token_count * top_count, dtype=jnp.int32)
    pair_live = pair_index // top_count < live_count
    expert_ids = jnp.arange(experts, dtype=jnp.int32)
    onehot = ((flat_routes[:, None] == expert_ids[None, :]) & pair_live[:, None]).astype(
        jnp.float32
    )
    before = jnp.cumsum(onehot, axis=0) - onehot
    position = jnp.sum(before * onehot, axis=1).astype(jnp.int32)
    target = (
        position // share_size * (experts * share_size)
        + flat_routes * share_size
        + position % share_size
    )
    slot_total = senders * experts * share_size
    placed = (target[None, :] == jnp.arange(slot_total, dtype=jnp.int32)[:, None]) & pair_live[
        None, :
    ]
    return (placed.astype(jnp.float32), jnp.sum(onehot, axis=0))


def on_device(tokens, hidden, routes, lengths):
    experts = lax.axis_size("expert")
    senders = lax.axis_size("dp")
    token_count = tokens.shape[0]
    top_count = routes.shape[1]
    share_size = (5 * token_count + 2 * experts * senders - 1) // (2 * experts * senders)
    placed, local_counts = dispatch_tables(routes, lengths[0], experts, share_size, senders)
    slot_total = placed.shape[0]
    by_token = jnp.sum(placed.reshape(slot_total, token_count, top_count), axis=2).astype(
        jnp.bfloat16
    )
    send_tokens = jnp.dot(by_token, tokens, preferred_element_type=jnp.float32).astype(jnp.bfloat16)
    flat_hidden = hidden.reshape(token_count * top_count, hidden.shape[2])
    send_hidden = jnp.dot(
        placed.astype(jnp.bfloat16), flat_hidden, preferred_element_type=jnp.float32
    ).astype(jnp.bfloat16)
    slot_tokens, slot_hidden = sent_together((send_tokens, send_hidden), ("dp", "expert"), 0, 0, 1)
    global_counts = of_everyone(local_counts, ("dp", "expert"))
    own_expert = lax.axis_index("expert")
    own_count = jnp.sum(
        jnp.where(jnp.arange(experts, dtype=jnp.int32) == own_expert, global_counts, 0.0)
    )
    factor = 2.0 / jnp.maximum(own_count, 1.0)
    full_tokens, full_hidden = (
        lax.all_gather(slot_tokens, "tile", axis=1, tiled=True),
        lax.all_gather(slot_hidden, "tile", axis=1, tiled=True),
    )
    column_tokens, column_hidden = (
        lax.all_to_all(full_tokens, "dp", split_axis=1, concat_axis=0, tiled=True),
        lax.all_to_all(full_hidden, "dp", split_axis=1, concat_axis=0, tiled=True),
    )
    pieces = side_by_side((slot_tokens, slot_hidden), "dp", 0, 1)
    gram_tokens = contract(pieces[0], column_tokens)
    gram_hidden = contract(pieces[1], column_hidden)
    return ((gram_tokens * factor)[None], (gram_hidden * factor)[None])


def solution(mesh):
    placed = (
        P(("dp", "expert"), "tile"),
        P(("dp", "expert"), None, "tile"),
        P(("dp", "expert"), None),
        P(("dp", "expert")),
    )
    return jax.shard_map(
        on_device,
        mesh=mesh,
        in_specs=placed,
        out_specs=(P("expert", "tile", "dp"), P("expert", "tile", "dp")),
        check_vma=False,
    )
```

profile of v0, /device:TPU:1, one launch (start us, length us, event | category | flops | bytes accessed | tf_op | source)
XLA Modules:
  0.0 226.2 jit_solution(10405702550066354825)
XLA Ops:
  7.9 0.8 copy.33
  8.7 0.1 eq.43
  8.8 0.1 fusion.11
  8.9 0.2 reduce_window_sum.11
  9.1 0.2 fusion.12
  9.3 0.1 rem.32
  9.5 0.1 div.25
  9.8 0.2 ne.82
  10.1 1.2 reshape.98
  11.2 0.7 fusion.18
  11.9 0.1 convert_reduce_fusion
  12.1 0.3 convolution_convert_fusion.1
  12.3 0.3 convolution_convert_fusion
  12.8 0.5 all_to_all.40
  13.3 49.6 %all_to_all.56 = bf16[64,3,2816]{2,1,0:T(4,128)(2,1)S(1)} all-to-all(bf16[64,3,2816]{2,1,0:T(4,128)(2,1)S(1)} %all_to_all.40), channel_id=1, replica_groups=mesh['dp'=8,'expert'=8,'tile'=4] {'dp','expert'}, dimensions={0} | all-to-all | bytes 2162688 | tf_op jit(solution)/shard_map/all_to_all | solution.py:10
  62.8 0.9 all_to_all.42
  63.8 1.0 split.19
  64.8 0.8 split.17
  65.7 0.7 all-gather.4.cloned.1.call-update
  66.4 0.6 broadcast_in_dim.18
  67.0 6.7 %all-to-all-start.2 = ((f32[64,1,8]{2,1,0:T(1,128)}), f32[64,1,8]{2,1,0:T(1,128)S(1)}, u32[]{:S(2)}, u32[]{:S(2)}) async-start(f32[64,1,8]{2,1,0:T(1,128)} %broadcast_in_dim.18), calls=%async_computation.2 | async-start | bytes 65536 | tf_op jit(solution)/shard_map/all_to_all | solution.py:16
  73.8 27.1 %all-gather.8.cloned.1.call-done = bf16[192,7168]{1,0:T(8,128)(2,1)} async-done(((bf16[192,1792]{1,0:T(8,128)(2,1)}), bf16[192,7168]{1,0:T(8,128)(2,1)}) %all-gather.8.cloned.1.call-update) | async-done | bytes 2752528 | tf_op jit(solution)/shard_map/all_gather | solution.py:88
  100.9 3.7 %copy.49 = bf16[24,8,8,896]{3,2,0,1:T(8,128)(2,1)} copy(bf16[24,8,8,896]{3,2,1,0:T(8,128)(2,1)} %bitcast.27) | data formatting | bytes 5505024 | tf_op jit(solution)/shard_map/all_to_all | solution.py:92
  104.6 5.1 %all-to-all-start.3 = ((bf16[192,8,896]{2,0,1:T(8,128)(2,1)}), bf16[192,8,896]{2,0,1:T(8,128)(2,1)S(1)}, u32[]{:S(2)}, u32[]{:S(2)}) async-start(bf16[192,8,896]{2,0,1:T(8,128)(2,1)} %bitcast.22), calls=%async_computation.3 | async-start | bytes 5505024 | tf_op jit(solution)/shard_map/all_to_all | solution.py:92
  109.7 22.2 %all-gather.6.cloned.1.call-done = bf16[192,4096]{1,0:T(8,128)(2,1)} async-done(((bf16[192,1024]{1,0:T(8,128)(2,1)}), bf16[192,4096]{1,0:T(8,128)(2,1)}) %all-gather.6.cloned.1.call-update) | async-done | bytes 1572880 | tf_op jit(solution)/shard_map/all_gather | solution.py:87
  131.9 2.7 %copy.50 = bf16[24,8,8,512]{3,2,0,1:T(8,128)(2,1)} copy(bf16[24,8,8,512]{3,2,1,0:T(8,128)(2,1)} %bitcast.28) | data formatting | bytes 3145728 | tf_op jit(solution)/shard_map/all_to_all | solution.py:91
  134.6 8.4 %all-to-all-done.3 = bf16[192,8,896]{2,0,1:T(8,128)(2,1)S(1)} async-done(((bf16[192,8,896]{2,0,1:T(8,128)(2,1)}), bf16[192,8,896]{2,0,1:T(8,128)(2,1)S(1)}, u32[]{:S(2)}, u32[]{:S(2)}) %all-to-all-start.3) | async-done | bytes 2752544 | tf_op jit(solution)/shard_map/all_to_all | solution.py:92
  142.9 5.2 %all-to-all-start.1 = ((bf16[192,8,512]{2,0,1:T(8,128)(2,1)}), bf16[192,8,512]{2,0,1:T(8,128)(2,1)}, u32[]{:S(2)}, u32[]{:S(2)}) async-start(bf16[192,8,512]{2,0,1:T(8,128)(2,1)} %bitcast.23), calls=%async_computation.1 | async-start | bytes 3145728 | tf_op jit(solution)/shard_map/all_to_all | solution.py:91
  148.2 0.6 fusion.22
  149.5 55.0 %all-gather.4.cloned.1.call-done = bf16[1536,2816]{1,0:T(8,128)(2,1)} async-done(((bf16[192,2816]{1,0:T(8,128)(2,1)}), bf16[1536,2816]{1,0:T(8,128)(2,1)}) %all-gather.4.cloned.1.call-update) | async-done | bytes 8650768 | tf_op jit(solution)/shard_map/all_gather | solution.py:30
  204.5 9.6 %multiply_bitcast_fusion = f32[1,1792,896]{2,1,0:T(8,128)} fusion(bf16[1536,896]{1,0:T(8,128)(2,1)S(1)} %bitcast.26, bf16[1536,2816]{1,0:T(8,128)(2,1)} %all-gather.4.cloned.1.call-done, f32[]{:T(128)S(6)} %div.27), kind=kOutput, calls=%fused_computation | convolution fusion | flops 4934107136 | bytes 14680068 | tf_op jit(solution)/shard_map/dot_general | solution.py:34
  214.2 5.5 %multiply_bitcast_fusion.1 = f32[1,1024,512]{2,1,0:T(8,128)} fusion(bf16[1536,512]{1,0:T(8,128)(2,1)} %bitcast.2, bf16[1536,2816]{1,0:T(8,128)(2,1)} %all-gather.4.cloned.1.call-done, f32[]{:T(128)S(6)} %div.27), kind=kOutput, calls=%fused_computation.7 | convolution fusion | flops 1611137024 | bytes 6815748 | tf_op jit(solution)/shard_map/dot_general | solution.py:34
  (20 shorter events, 0.6 us)
Async XLA Ops:
  7.2 4.9 %copy-start = (bf16[64,1024]{1,0:T(8,128)(2,1)S(1)}, bf16[64,1024]{1,0:T(8,128)(2,1)}, u32[]{:S(2)}) copy-start(bf16[64,1024]{1,0:T(8,128)(2,1)} %param.4) | copy-start | bytes 393220
  7.2 93.7 %all-gather.8.cloned.1.call-start = ((), (), s32[]{:S(2)}) async-start(), calls=%async_computation.6 | async-start | bytes 3440640 | tf_op jit(solution)/shard_map/all_gather | solution.py:88
  63.8 2.0 copy-start.1
  64.8 67.1 %all-gather.6.cloned.1.call-start = ((), (), s32[]{:S(2)}) async-start(), calls=%async_computation.5 | async-start | bytes 1966080 | tf_op jit(solution)/shard_map/all_gather | solution.py:87
  65.7 138.8 %all-gather.4.cloned.1.call-start = ((), (), s32[]{:S(2)}) async-start(), calls=%async_computation.4 | async-start | bytes 9732096 | tf_op jit(solution)/shard_map/all_gather | solution.py:30
  67.0 37.5 %all-to-all-start.2 = ((f32[64,1,8]{2,1,0:T(1,128)}), f32[64,1,8]{2,1,0:T(1,128)S(1)}, u32[]{:S(2)}, u32[]{:S(2)}) async-start(f32[64,1,8]{2,1,0:T(1,128)} %broadcast_in_dim.18), calls=%async_computation.2 | async-start | bytes 65536 | tf_op jit(solution)/shard_map/all_to_all | solution.py:16
  104.6 38.4 %all-to-all-start.3 = ((bf16[192,8,896]{2,0,1:T(8,128)(2,1)}), bf16[192,8,896]{2,0,1:T(8,128)(2,1)S(1)}, u32[]{:S(2)}, u32[]{:S(2)}) async-start(bf16[192,8,896]{2,0,1:T(8,128)(2,1)} %bitcast.22), calls=%async_computation.3 | async-start | bytes 5505024 | tf_op jit(solution)/shard_map/all_to_all | solution.py:92
  142.9 71.2 %all-to-all-start.1 = ((bf16[192,8,512]{2,0,1:T(8,128)(2,1)}), bf16[192,8,512]{2,0,1:T(8,128)(2,1)}, u32[]{:S(2)}, u32[]{:S(2)}) async-start(bf16[192,8,512]{2,0,1:T(8,128)(2,1)} %bitcast.23), calls=%async_computation.1 | async-start | bytes 3145728 | tf_op jit(solution)/shard_map/all_to_all | solution.py:91
Sparse Core Ops, SparseCore 0:
  64.9 35.9 all-gather.7
  102.7 29.1 all-gather.5
  133.7 70.7 all-gather.3
where the time goes:
time: 227 us; the launch traced here: 226 us
  waiting for transfers between devices  113 us (50%)
  blocking collectives  49.6 us (22%)
  starting transfers between devices  17.1 us (8%)
  matrix products  15.8 us (7%)
  between operations  15.3 us (7%)
  local copies, waits for them, and re-layouts  13 us (6%)
    all_gather x1, waiting for transfers between devices, side_by_side(): lax.all_gather(both, axis, axis=dim, tiled=True)  55 us
    all_to_all x1, blocking collectives, sent_together(): lax.all_to_all(both, axis, split_axis=split_dim, concat_axis=concat_dim,...  49.6 us
    all_gather x1, waiting for transfers between devices, on_device(): lax.all_gather(slot_hidden, 'tile', axis=1, tiled=True)  27.1 us
    all_gather x1, waiting for transfers between devices, on_device(): lax.all_gather(slot_tokens, 'tile', axis=1, tiled=True)  22.2 us
    dot_general x2, matrix products, contract(): lax.dot_general(left, right, (((0,), (0,)), ((), ())), preferred_element_...  15.2 us
    all_to_all x1, waiting for transfers between devices, on_device(): lax.all_to_all(full_hidden, 'dp', split_axis=1, concat_axis=0, tiled=True)  8.35 us
    all_to_all x1, starting transfers between devices, from_everyone(): return lax.all_to_all(copies, axis, split_axis=0, concat_axis=0, tiled=True)  6.72 us
    all_to_all x1, starting transfers between devices, on_device(): lax.all_to_all(full_tokens, 'dp', split_axis=1, concat_axis=0, tiled=True)  5.17 us
  transfers between devices with their start and end apart: 6, of which 4 were waited for; matrix products, arithmetic and copies ran while one was open for 8% of the time, Pallas kernels for 0%

commit v1 on v0

--- a/solution.py
+++ b/solution.py
@@ -1,7 +1,21 @@
+import functools
 import jax
 import jax.numpy as jnp
 from jax import lax
 from jax.sharding import PartitionSpec as P
+from jax.lax import all_to_all, psum
+
+
+def heads_deliver(row_data, axis_no):
+    xs_all = []
+    for _ in range(psum(1, axis_name="tile")):
+        xs_all.append(row_data)
+    return jnp.concatenate(
+        all_to_all(jnp.stack(xs_all), axis_name="tile", split_axis=0, concat_axis=0), axis=axis_no
+    )
+
+
+serve_links_by_axis = functools.partial(heads_deliver, axis_no=1)
 
 
 def sent_together(arrays, axis, split_dim, concat_dim, along):
@@ -85,7 +99,7 @@
     factor = 2.0 / jnp.maximum(own_count, 1.0)
     full_tokens, full_hidden = (
         lax.all_gather(slot_tokens, "tile", axis=1, tiled=True),
-        lax.all_gather(slot_hidden, "tile", axis=1, tiled=True),
+        serve_links_by_axis(slot_hidden),
     )
     column_tokens, column_hidden = (
         lax.all_to_all(full_tokens, "dp", split_axis=1, concat_axis=0, tiled=True),

time: 227 us -> 234 us (1.031)
  waiting for transfers between devices: 113 us -> 63.8 us
  blocking collectives: 49.6 us -> 98.4 us
  local copies, waits for them, and re-layouts: 13 us -> 20.1 us
    all_gather x1, waiting for transfers between devices: 55 us -> 0.02 us  [side_by_side(): lax.all_gather(both, axis, axis=dim, tiled=True)]
    all_to_all x0 -> x1, blocking collectives: none -> 48.9 us  [heads_deliver(): all_to_all(jnp.stack(xs_all), axis_name='tile', split_axis=0, concat_axis=0)]
    all_to_all x1, waiting for transfers between devices: 8.35 us -> 53.5 us  [on_device(): lax.all_to_all(full_hidden, 'dp', split_axis=1, concat_axis=0, tiled=True)]
    all_gather x1 -> x0, waiting for transfers between devices: 27.1 us -> none  [on_device(): lax.all_gather(slot_hidden, 'tile', axis=1, tiled=True)]
    all_gather x1, waiting for transfers between devices: 22.2 us -> 0.01 us  [on_device(): lax.all_gather(slot_tokens, 'tile', axis=1, tiled=True)]
    all_to_all x1, waiting for transfers between devices: 0.01 us -> 9.72 us  [on_device(): lax.all_to_all(full_tokens, 'dp', split_axis=1, concat_axis=0, tiled=True)]
    reshape x0 -> x1, local copies, waits for them, and re-layouts: none -> 3.66 us  [heads_deliver(): jnp.concatenate(all_to_all(jnp.stack(xs_all), axis_name='tile', split_axi...]
    all_to_all x1 -> x2, local copies, waits for them, and re-layouts: 3.69 us -> 6.57 us  [on_device(): lax.all_to_all(full_hidden, 'dp', split_axis=1, concat_axis=0, tiled=True)]
  transfers between devices with their start and end apart: 6 -> 5, of which waited for: 4 -> 2; matrix products, arithmetic and copies ran while one was open for 8% -> 9% of each run, Pallas kernels for 0% -> 0%
where the time goes in v1:
time: 234 us; the launch traced here: 233 us
  blocking collectives  98.4 us (42%)
  waiting for transfers between devices  63.8 us (27%)
  local copies, waits for them, and re-layouts  20.1 us (9%)
  starting transfers between devices  17.6 us (8%)
  matrix products  15.7 us (7%)
  between operations  15.6 us (7%)
    all_to_all x1, waiting for transfers between devices, on_device(): lax.all_to_all(full_hidden, 'dp', split_axis=1, concat_axis=0, tiled=True)  53.5 us
    all_to_all x1, blocking collectives, sent_together(): lax.all_to_all(both, axis, split_axis=split_dim, concat_axis=concat_dim,...  49.6 us
    all_to_all x1, blocking collectives, heads_deliver(): all_to_all(jnp.stack(xs_all), axis_name='tile', split_axis=0, concat_axis=0)  48.9 us
    dot_general x2, matrix products, contract(): lax.dot_general(left, right, (((0,), (0,)), ((), ())), preferred_element_...  15.1 us
    all_to_all x1, waiting for transfers between devices, on_device(): lax.all_to_all(full_tokens, 'dp', split_axis=1, concat_axis=0, tiled=True)  9.72 us
    all_to_all x1, starting transfers between devices, from_everyone(): return lax.all_to_all(copies, axis, split_axis=0, concat_axis=0, tiled=True)  7.91 us
    all_to_all x2, local copies, waits for them, and re-layouts, on_device(): lax.all_to_all(full_hidden, 'dp', split_axis=1, concat_axis=0, tiled=True)  6.57 us
    all_to_all x1, starting transfers between devices, on_device(): lax.all_to_all(full_hidden, 'dp', split_axis=1, concat_axis=0, tiled=True)  4.9 us
  transfers between devices with their start and end apart: 5, of which 2 were waited for; matrix products, arithmetic and copies ran while one was open for 9% of the time, Pallas kernels for 0%

profile of v1, /device:TPU:1, one launch (start us, length us, event | category | flops | bytes accessed | tf_op | source)
XLA Modules:
  0.0 233.3 jit_solution(17416433230416607905)
XLA Ops:
  7.9 0.8 copy.42
  8.7 0.1 eq.43
  8.9 0.2 reduce_window_sum.11
  9.1 0.2 fusion.12
  9.5 0.1 div.25
  9.8 0.2 ne.82
  10.1 1.2 reshape.105
  11.2 0.7 fusion.18
  12.1 0.3 convolution_convert_fusion.1
  12.4 0.3 convolution_convert_fusion
  12.8 0.5 all_to_all.43
  13.3 49.6 %all_to_all.61 = bf16[64,3,2816]{2,1,0:T(4,128)(2,1)S(1)} all-to-all(bf16[64,3,2816]{2,1,0:T(4,128)(2,1)S(1)} %all_to_all.43), channel_id=1, replica_groups=mesh['dp'=8,'expert'=8,'tile'=4] {'dp','expert'}, dimensions={0} | all-to-all | bytes 2162688 | tf_op jit(solution)/shard_map/all_to_all | solution.py:24
  62.8 0.9 all_to_all.45
  63.8 0.9 split.17
  64.7 0.2 copy-done.1
  64.9 0.5 all-gather.3.cloned.1.call-update
  65.4 1.1 split.19
  66.6 0.2 stack.2
  66.7 48.9 %all_to_all.62 = bf16[4,192,1792]{2,1,0:T(8,128)(2,1)S(1)} all-to-all(bf16[4,192,1792]{2,1,0:T(8,128)(2,1)S(1)} %stack.2), channel_id=1, replica_groups=mesh['dp'=8,'expert'=8,'tile'=4] {'tile'}, dimensions={0} | all-to-all | bytes 5505024 | tf_op jit(solution)/shard_map/all_to_all | solution.py:14
  115.6 0.6 broadcast_in_dim.18
  116.2 7.9 %all-to-all-start.2 = ((f32[64,1,8]{2,1,0:T(1,128)}), f32[64,1,8]{2,1,0:T(1,128)S(1)}, u32[]{:S(2)}, u32[]{:S(2)}) async-start(f32[64,1,8]{2,1,0:T(1,128)} %broadcast_in_dim.18), calls=%async_computation.2 | async-start | bytes 65536 | tf_op jit(solution)/shard_map/all_to_all | solution.py:30
  124.2 3.7 %copy.52 = bf16[192,4,1792]{2,1,0:T(4,128)(2,1)} copy(bf16[192,4,1792]{2,0,1:T(8,128)(2,1)S(1)} %bitcast.23) | data formatting | bytes 5505024 | tf_op jit(solution)/shard_map/reshape | solution.py:13
  127.8 4.6 %all_to_all.52 = bf16[192,8,896]{2,1,0:T(8,128)(2,1)S(1)} reshape(bf16[192,4,1792]{2,1,0:T(4,128)(2,1)} %copy.52) | data formatting | bytes 5505024 | tf_op jit(solution)/shard_map/all_to_all | solution.py:106
  132.4 2.0 copy.53
  134.4 4.9 %all-to-all-start.4 = ((bf16[192,8,896]{2,0,1:T(8,128)(2,1)}), bf16[192,8,896]{2,0,1:T(8,128)(2,1)S(1)}, u32[]{:S(2)}, u32[]{:S(2)}) async-start(bf16[192,8,896]{2,0,1:T(8,128)(2,1)} %copy.53), calls=%async_computation.4 | async-start | bytes 5505024 | tf_op jit(solution)/shard_map/all_to_all | solution.py:106
  139.3 2.7 %copy.57 = bf16[24,8,8,512]{3,2,0,1:T(8,128)(2,1)} copy(bf16[24,8,8,512]{3,2,1,0:T(8,128)(2,1)} %bitcast.25) | data formatting | bytes 3145728 | tf_op jit(solution)/shard_map/all_to_all | solution.py:105
  142.0 53.5 %all-to-all-done.4 = bf16[192,8,896]{2,0,1:T(8,128)(2,1)S(1)} async-done(((bf16[192,8,896]{2,0,1:T(8,128)(2,1)}), bf16[192,8,896]{2,0,1:T(8,128)(2,1)S(1)}, u32[]{:S(2)}, u32[]{:S(2)}) %all-to-all-start.4) | async-done | bytes 2752544 | tf_op jit(solution)/shard_map/all_to_all | solution.py:106
  195.5 4.7 %all-to-all-start.1 = ((bf16[192,8,512]{2,0,1:T(8,128)(2,1)}), bf16[192,8,512]{2,0,1:T(8,128)(2,1)}, u32[]{:S(2)}, u32[]{:S(2)}) async-start(bf16[192,8,512]{2,0,1:T(8,128)(2,1)} %bitcast.20), calls=%async_computation.1 | async-start | bytes 3145728 | tf_op jit(solution)/shard_map/all_to_all | solution.py:105
  200.3 0.6 fusion.22
  201.6 9.6 %multiply_bitcast_fusion = f32[1,1792,896]{2,1,0:T(8,128)} fusion(bf16[1536,896]{1,0:T(8,128)(2,1)S(1)} %bitcast.24, bf16[1536,2816]{1,0:T(8,128)(2,1)} %all-gather.3.cloned.1.call-done, f32[]{:T(128)S(6)} %div.27), kind=kOutput, calls=%fused_computation | convolution fusion | flops 4934107136 | bytes 14680068 | tf_op jit(solution)/shard_map/dot_general | solution.py:48
  211.2 9.7 %all-to-all-done.1 = bf16[192,8,512]{2,0,1:T(8,128)(2,1)} async-done(((bf16[192,8,512]{2,0,1:T(8,128)(2,1)}), bf16[192,8,512]{2,0,1:T(8,128)(2,1)}, u32[]{:S(2)}, u32[]{:S(2)}) %all-to-all-start.1) | async-done | bytes 1572896 | tf_op jit(solution)/shard_map/all_to_all | solution.py:105
  221.0 5.5 %multiply_bitcast_fusion.1 = f32[1,1024,512]{2,1,0:T(8,128)} fusion(bf16[1536,512]{1,0:T(8,128)(2,1)} %bitcast.2, bf16[1536,2816]{1,0:T(8,128)(2,1)} %all-gather.3.cloned.1.call-done, f32[]{:T(128)S(6)} %div.27), kind=kOutput, calls=%fused_computation.6 | convolution fusion | flops 1611137024 | bytes 6815748 | tf_op jit(solution)/shard_map/dot_general | solution.py:48
  (21 shorter events, 0.9 us)
Async XLA Ops:
  7.2 4.9 %copy-start = (bf16[64,1024]{1,0:T(8,128)(2,1)S(1)}, bf16[64,1024]{1,0:T(8,128)(2,1)}, u32[]{:S(2)}) copy-start(bf16[64,1024]{1,0:T(8,128)(2,1)} %param.4) | copy-start | bytes 393220
  7.2 132.1 %all-gather.5.cloned.1.call-start = ((), (), s32[]{:S(2)}) async-start(), calls=%async_computation.6 | async-start | bytes 1966080 | tf_op jit(solution)/shard_map/all_gather | solution.py:101
  63.8 1.1 copy-start.1
  64.7 137.0 %all-gather.3.cloned.1.call-start = ((), (), s32[]{:S(2)}) async-start(), calls=%async_computation.5 | async-start | bytes 9732096 | tf_op jit(solution)/shard_map/all_gather | solution.py:44
  116.2 18.2 %all-to-all-start.2 = ((f32[64,1,8]{2,1,0:T(1,128)}), f32[64,1,8]{2,1,0:T(1,128)S(1)}, u32[]{:S(2)}, u32[]{:S(2)}) async-start(f32[64,1,8]{2,1,0:T(1,128)} %broadcast_in_dim.18), calls=%async_computation.2 | async-start | bytes 65536 | tf_op jit(solution)/shard_map/all_to_all | solution.py:30
  134.4 61.1 %all-to-all-start.4 = ((bf16[192,8,896]{2,0,1:T(8,128)(2,1)}), bf16[192,8,896]{2,0,1:T(8,128)(2,1)S(1)}, u32[]{:S(2)}, u32[]{:S(2)}) async-start(bf16[192,8,896]{2,0,1:T(8,128)(2,1)} %copy.53), calls=%async_computation.4 | async-start | bytes 5505024 | tf_op jit(solution)/shard_map/all_to_all | solution.py:106
  195.5 25.4 %all-to-all-start.1 = ((bf16[192,8,512]{2,0,1:T(8,128)(2,1)}), bf16[192,8,512]{2,0,1:T(8,128)(2,1)}, u32[]{:S(2)}, u32[]{:S(2)}) async-start(bf16[192,8,512]{2,0,1:T(8,128)(2,1)} %bitcast.20), calls=%async_computation.1 | async-start | bytes 3145728 | tf_op jit(solution)/shard_map/all_to_all | solution.py:105
Sparse Core Ops, SparseCore 0:
  64.8 51.0 all-gather.4
  117.7 72.3 all-gather.2
